TPU v7x, 32 devices: a whole 2x2x4 slice. The times are simulated.
32 devices in a mesh: row: 8 (over z, x), col: 4 (over y, core).
Axes of the slice: x: 2, y: 2, z: 4, core: 2. Of those that a mesh axis runs over, the one named last changes fastest.
Arguments:
- sparse_blocks: float32 [4096, 128, 128], P(('row', 'col')), may hold values from -0.5 to 0.5
- panel_rows: float32 [262144, 128], P(('row', 'col')), may hold values from -6 to 6
- block_row: int32 [4096], P(('row', 'col')), may hold values from 0 to 63
- block_owner: int32 [4096, 1], P(('row', 'col')), may hold values from 0 to 31; in each aligned block of 128 rows (0 to 127, 128 to 255, ...) at most 8 rows name the same one
- block_offset: int32 [4096], P(('row', 'col')), may hold values from 0 to 63
Outputs:
- result: float32 [262144, 128], P(('row', 'col'))
Inputs may be any that keep to these rules, and one draw needn't show every extreme that they name: `block_owner`: among the blocks of one device, at most 8 name the same owner, a bound that some block reaches.
All inputs are finite; a program needn't handle non-finite values.
Results may differ from a plain program's by a relative error of at most 0.0001.
Values sent between devices are 32-bit elements; how exact they have to be, the bound alone decides.
A program may use at most 192 MiB of HBM per device.

v0:
```python
import functools

import jax
import jax.numpy as jnp
from jax import lax
from jax.experimental import pallas as pl
from jax.experimental.pallas import tpu as pltpu
from jax.sharding import PartitionSpec as P

AXES = ("row", "col")
VMEM_LIMIT = 67_000_000
LANES = 128
TILE = 8
MESH = pl.DeviceIdType.MESH


def split_parts(value):
    high = value.astype(jnp.bfloat16)
    low = (value - high.astype(jnp.float32)).astype(jnp.bfloat16)
    return high, low


def block_product(block, panel):
    block_high, block_low = split_parts(block)
    panel_high, panel_low = split_parts(panel)
    dims = (((0,), (0,)), ((), ()))
    dot = functools.partial(lax.dot_general, dimension_numbers=dims, preferred_element_type=jnp.float32)
    return dot(
        jnp.concatenate([block_high, block_low], axis=0),
        jnp.concatenate([panel_high, panel_high], axis=0),
    ) + dot(block_high, panel_low)


def peers_of(upper, lower, outer):
    moves = [
        (a, b, c) for a in range(upper) for b in range(lower) for c in range(outer) if (a, b, c) != (0, 0, 0)
    ]
    single = [move for move in moves if sum(digit > 0 for digit in move) == 1]
    double = [move for move in moves if sum(digit > 0 for digit in move) == 2]
    zeros = lambda move: tuple(digit == 0 for digit in move)
    order = sorted(single, key=zeros)
    opposite = sorted(double, key=lambda move: tuple(digit > 0 for digit in move))
    pairs = list(zip(order, opposite))
    first = [one for one, _ in pairs] + [other for _, other in pairs]
    second = [other for _, other in pairs] + [one for one, _ in pairs]
    rest = [move for move in moves if move not in first]
    return first + rest, second + rest


def route_kernel(
    row_half,
    per_owner,
    source_ref,
    panel_at_ref,
    keep_ref,
    sparse_hbm,
    panel_hbm,
    table_hbm,
    out_hbm,
    sparse,
    panel,
    products,
    far_land,
    near_land,
    sums,
    crossed,
    total,
    tables,
    near_table,
    far_table,
    data_send,
    data_recv,
    table_send,
    table_recv,
    cross_send,
    cross_recv,
    load_sems,
    own_sems,
    out_sems,
):
    row, col = lax.axis_index("row"), lax.axis_index("col")
    row_count, col_count = lax.axis_size("row"), lax.axis_size("col")
    half, inner = row // row_half, row % row_half
    outer, core = col // 2, col % 2
    lower = min(2, row_half)
    mine = inner * col_count + col
    count = row_half * col_count
    half_slots = count * per_owner
    upper_count, outer_count = row_half // lower, col_count // 2
    local_blocks = total.shape[0]
    chunk = min(8, local_blocks)
    chunks = local_blocks // chunk

    loads = [
        pltpu.make_async_copy(sparse_hbm, sparse, load_sems.at[0]),
        pltpu.make_async_copy(panel_hbm, panel, load_sems.at[1]),
    ]
    for load in loads:
        load.start()
    blank = jnp.zeros(far_land.shape[1:], jnp.float32)
    far_land[half_slots] = blank
    near_land[half_slots] = blank

    def target(move_pair, flip):
        one, other = move_pair
        a, b, c = (x + core * (y - x) for x, y in zip(one, other))
        there = (inner // lower + a) % upper_count * lower + (inner % lower + b) % lower
        beside = (outer + c) % outer_count * 2 + (core + flip) % 2
        number = ((a * lower + b) * outer_count + c) * 2 + flip
        return (half * row_half + there, beside), there * col_count + beside, number

    firsts, seconds = peers_of(upper_count, lower, outer_count)
    moves = list(zip(firsts, seconds))
    still = ((0, 0, 0), (0, 0, 0))
    targets = [target(move, (core + phase) % 2) for phase in range(2) for move in moves]
    targets.append(target(still, 1))
    opposite = ((row + row_half) % row_count, col)

    barrier = pltpu.get_barrier_semaphore()
    for device, _, _ in targets:
        pl.semaphore_signal(barrier, inc=1, device_id=device, device_id_type=MESH)
    pl.semaphore_signal(barrier, inc=1, device_id=opposite, device_id_type=MESH)
    pl.semaphore_wait(barrier, len(targets) + 1)

    def remote(source, destination, send_sem, recv_sem, device):
        copy = pltpu.make_async_remote_copy(
            src_ref=source,
            dst_ref=destination,
            send_sem=send_sem,
            recv_sem=recv_sem,
            device_id=device,
            device_id_type=MESH,
        )
        copy.start()
        return copy

    table_copies = [
        remote(table_hbm.at[place], tables.at[mine], table_send.at[number], table_recv.at[number], device)
        for device, place, number in targets
    ]
    own_table = pltpu.make_async_copy(table_hbm.at[mine], tables.at[mine], own_sems.at[0])
    own_table.start()
    for load in loads:
        load.wait()

    unit = min(4, per_owner)

    def fill(base, place, destination, at):
        first = base + place * per_owner

        def some(step, _):
            for k in range(unit):
                slot = step * unit + k
                source = source_ref[first + slot]
                product = block_product(sparse[source], panel[panel_at_ref[first + slot]])
                before = destination[at + jnp.maximum(slot - 1, 0)]
                product = product + jnp.where(keep_ref[first + slot] > 0, before, 0.0)
                destination[at + slot] = product
            return 0

        lax.fori_loop(0, per_owner // unit, some, 0)

    def spread(base, land, shift):
        copies = []
        for device, place, number in targets:
            at = base + place * per_owner
            fill(base, place, products, at)
            copies.append(
                remote(
                    products.at[pl.ds(at, per_owner)],
                    land.at[pl.ds(mine * per_owner, per_owner)],
                    data_send.at[shift + number],
                    data_recv.at[shift + number],
                    device,
                )
            )
        fill(base, mine, land, mine * per_owner)
        return copies

    far_copies = spread(half_slots, far_land, count)
    near_copies = spread(0, near_land, 0)

    own_table.wait()
    for copy in table_copies:
        copy.wait_recv()
    lookups = [
        pltpu.make_async_copy(tables.at[:, 0, :], near_table, own_sems.at[1]),
        pltpu.make_async_copy(tables.at[:, TILE, :], far_table, own_sems.at[2]),
    ]
    for lookup in lookups:
        lookup.start()
    for lookup in lookups:
        lookup.wait()

    def reduce(land, table, destination, first, number):
        def one(step, _):
            column = first + step
            value = land[table[0, column]]
            for origin in range(1, count):
                value = value + land[table[origin, column]]
            destination[column] = value
            return 0

        lax.fori_loop(0, number, one, 0)

    for copy in far_copies:
        copy.wait_recv()
    cross_copies = []
    for index in range(chunks):
        reduce(far_land, far_table, sums, index * chunk, chunk)
        part = pl.ds(index * chunk, chunk)
        cross_copies.append(
            remote(sums.at[part], crossed.at[part], cross_send.at[index], cross_recv.at[index], opposite)
        )
    for copy in near_copies:
        copy.wait_recv()
    reduce(near_land, near_table, total, 0, local_blocks)
    outs = []
    for index, copy in enumerate(cross_copies):
        copy.wait_recv()
        part = pl.ds(index * chunk, chunk)
        total[part] = total[part] + crossed[part]
        out = pltpu.make_async_copy(total.at[part], out_hbm.at[part], out_sems.at[index])
        out.start()
        outs.append(out)
    for copy in table_copies + far_copies + near_copies + cross_copies:
        copy.wait_send()
    for out in outs:
        out.wait()


def route(source, panel_at, keep, sparse_blocks, panel_blocks, table, row_half, per_owner):
    count = row_half * lax.axis_size("col")
    local_blocks, size, width = panel_blocks.shape
    half_slots = count * per_owner
    chunks = local_blocks // min(8, local_blocks)
    lanes = table.shape[-1]
    scalars = pl.BlockSpec(memory_space=pltpu.SMEM)
    anywhere = pl.BlockSpec(memory_space=pl.ANY)
    block = (size, width)
    dma = pltpu.SemaphoreType.DMA
    return pl.pallas_call(
        functools.partial(route_kernel, row_half, per_owner),
        in_specs=[scalars] * 3 + [anywhere] * 3,
        out_specs=anywhere,
        out_shape=jax.ShapeDtypeStruct((local_blocks,) + block, jnp.float32),
        scratch_shapes=[
            pltpu.VMEM(sparse_blocks.shape, jnp.float32),
            pltpu.VMEM(panel_blocks.shape, jnp.float32),
            pltpu.VMEM((2 * half_slots,) + block, jnp.float32),
            pltpu.VMEM((half_slots + 1,) + block, jnp.float32),
            pltpu.VMEM((half_slots + 1,) + block, jnp.float32),
            pltpu.VMEM((local_blocks,) + block, jnp.float32),
            pltpu.VMEM((local_blocks,) + block, jnp.float32),
            pltpu.VMEM((local_blocks,) + block, jnp.float32),
            pltpu.VMEM((count, 2 * TILE, lanes), jnp.int32),
            pltpu.SMEM((count, lanes), jnp.int32),
            pltpu.SMEM((count, lanes), jnp.int32),
            dma((2 * count,)),
            dma((2 * count,)),
            dma((count,)),
            dma((count,)),
            dma((chunks,)),
            dma((chunks,)),
            dma((2,)),
            dma((3,)),
            dma((chunks,)),
        ],
        compiler_params=pltpu.CompilerParams(
            collective_id=0, has_side_effects=True, vmem_limit_bytes=VMEM_LIMIT
        ),
    )(source, panel_at, keep, sparse_blocks, panel_blocks, table)


def body(sparse_blocks, panel_rows, block_row, block_owner, block_offset):
    device_count = lax.axis_size("row") * lax.axis_size("col")
    half_count = device_count // 2
    slot_count, size, _ = sparse_blocks.shape
    width = panel_rows.shape[1]
    local_blocks = panel_rows.shape[0] // size
    per_owner = max(2, 2 * slot_count // device_count)
    half_slots = half_count * per_owner
    me = lax.axis_index(AXES)
    my_half = me // half_count
    row_half = lax.axis_size("row") // 2
    owner = block_owner[:, 0]
    index = jnp.arange(slot_count, dtype=jnp.int32)
    key = block_offset * slot_count + index
    same = owner[:, None] == owner[None, :]
    earlier = same & (key[None, :] < key[:, None])
    order = jnp.sum(earlier.astype(jnp.int32), axis=1)
    again = jnp.any(earlier & (block_offset[None, :] == block_offset[:, None]), axis=1).astype(jnp.int32)
    half_of = (owner // half_count != my_half).astype(jnp.int32)
    group = half_of * half_count + owner % half_count
    position = group * per_owner + order
    hit = position[None, :] == jnp.arange(2 * half_slots, dtype=jnp.int32)[:, None]
    pick = lambda value: jnp.max(jnp.where(hit, value[None, :], 0), axis=1)
    source, panel_at, keep = pick(index), pick(block_row), pick(again)

    lanes = -(-local_blocks // LANES) * LANES
    place = (me % half_count) * per_owner + order
    cell = (group[None, :] == jnp.arange(2 * half_count, dtype=jnp.int32)[:, None])[:, None, :] & (
        block_offset[None, :] == jnp.arange(lanes, dtype=jnp.int32)[:, None]
    )[None]
    table = jnp.max(jnp.where(cell, place[None, None, :], -1), axis=2)
    table = jnp.where(table < 0, half_slots, table)
    table = table.reshape(2, half_count, 1, lanes).transpose(1, 0, 2, 3)
    table = jnp.broadcast_to(table, (half_count, 2, TILE, lanes)).reshape(half_count, 2 * TILE, lanes)

    panel_blocks = panel_rows.reshape(local_blocks, size, width)
    total = route(source, panel_at, keep, sparse_blocks, panel_blocks, table, row_half, per_owner)
    return total.reshape(local_blocks * size, width)


def solution(mesh):
    placed = (
        P(AXES, None, None),
        P(AXES, None),
        P(AXES),
        P(AXES, None),
        P(AXES),
    )
    return jax.shard_map(
        body, mesh=mesh, in_specs=placed, out_specs=P(AXES, None), check_vma=False
    )
```

profile of v0, /device:TPU:1, one launch (start us, length us, event | category | flops | bytes accessed | tf_op | source)
XLA Modules:
  0.0 298.6 jit_solution(8368114046366610476)
XLA Ops:
  0.0 0.7 iota_add_fusion
  0.7 0.9 convert_reduce_fusion
  1.6 0.7 multiply_add_fusion
  2.3 0.9 iota_compare_fusion.1
  3.2 0.6 select_reduce_fusion
  3.9 1.4 select_reduce_fusion.1
  5.3 0.7 broadcast_bitcast_fusion.table_hbm
  6.0 288.1 %shard_map.55 = f32[64,128,128]{2,1,0:T(8,128)} custom-call(s32[256]{0:T(256)} %get-tuple-element.7.source_ref, s32[256]{0:T(256)} %get-tuple-element.6.panel_at_ref, s32[256]{0:T(256)} %get-tuple-element.5.keep_ref, f32[128,128,128]{2,1,0:T(8,128)} %sparse_hbm.1, f32[64,128,128]{2,1,0:T(8,128)} %bitcast.13, s32[16,16,128]{2,1,0:T(8,128)} %broadcast_bitcast_fusion.table_hbm), custom_call_target="tpu_custom_call" | custom-call | tf_op jit(solution)/shard_map/pallas_call | solution.py:242
  294.1 4.5 %copy.9 = f32[8192,128]{1,0:T(8,128)} copy(f32[8192,128]{1,0:T(8,128)} %bitcast.12) | data formatting | bytes 8388608
  (4 shorter events, 0.0 us)
where the time goes:
time: 299 us
  Pallas kernels  288 us (96%)
  other arithmetic  5.24 us (2%)
  local copies, waits for them, and re-layouts  5.14 us (2%)
    pallas_call x1, Pallas kernels, route(): pl.pallas_call(functools.partial(route_kernel, row_half, per_owner), in_s...  288 us

commit v1 on v0

--- a/solution.py
+++ b/solution.py
@@ -11,6 +11,7 @@
 VMEM_LIMIT = 67_000_000
 LANES = 128
 TILE = 8
+SPILL = 1 << 20
 MESH = pl.DeviceIdType.MESH
 
 
@@ -272,6 +273,398 @@
     )(source, panel_at, keep, sparse_blocks, panel_blocks, table)
 
 
+def layer_kernel(
+    row_half,
+    per_owner,
+    first_list,
+    slot_ref,
+    sparse_hbm,
+    panel_hbm,
+    table_hbm,
+    out_hbm,
+    flag_ref,
+    sparse,
+    panel,
+    products,
+    far_land,
+    near_land,
+    list_one,
+    list_two,
+    sums,
+    crossed,
+    total,
+    tables,
+    spill,
+    spill_in,
+    near_table,
+    far_table,
+    starts,
+    far_send,
+    far_recv,
+    near_send,
+    near_recv,
+    pass_send,
+    pass_recv,
+    list_send,
+    list_recv,
+    table_send,
+    table_recv,
+    cross_send,
+    cross_recv,
+    spill_sems,
+    load_sems,
+    own_sems,
+    out_sems,
+):
+    row, col = lax.axis_index("row"), lax.axis_index("col")
+    row_count, col_count = lax.axis_size("row"), lax.axis_size("col")
+    half, inner = row // row_half, row % row_half
+    outer, core = col // 2, col % 2
+    lower = min(2, row_half)
+    layer, beside_x = inner // lower, inner % lower
+    mine = inner * col_count + col
+    count = row_half * col_count
+    around = lower * col_count
+    half_slots = count * per_owner
+    outer_count = col_count // 2
+    rows_of_panel = panel.shape[0]
+    local_blocks = total.shape[0]
+    chunk = min(8, local_blocks)
+    chunks = local_blocks // chunk
+    second_list = list_two.shape[0]
+    near_base, far_base, list_base = 0, around * per_owner, around * per_owner + half_slots
+
+    loads = [
+        pltpu.make_async_copy(sparse_hbm, sparse, load_sems.at[0]),
+        pltpu.make_async_copy(panel_hbm, panel, load_sems.at[1]),
+    ]
+    for load in loads:
+        load.start()
+    blank = jnp.zeros(far_land.shape[1:], jnp.float32)
+    far_land[half_slots] = blank
+    near_land[half_slots] = blank
+
+    def target(move_pair, flip):
+        one, other = move_pair
+        a, b, c = (x + core * (y - x) for x, y in zip(one, other))
+        there = (layer + a) % 2 * lower + (beside_x + b) % lower
+        beside = (outer + c) % outer_count * 2 + (core + flip) % 2
+        number = ((a * lower + b) * outer_count + c) * 2 + flip
+        return (half * row_half + there, beside), there * col_count + beside, number
+
+    firsts, seconds = peers_of(2, lower, outer_count)
+    moves = list(zip(firsts, seconds))
+    flat = [move for move in firsts if move[0] == 0]
+    flat_moves = list(zip(flat, sorted(flat, key=lambda move: (sum(move), move[1]))))
+    still = ((0, 0, 0), (0, 0, 0))
+    sibling = target(still, 1)
+    partner_inner = (layer + 1) % 2 * lower + beside_x
+    partner, partner_place = (half * row_half + partner_inner, col), partner_inner * col_count + col
+    opposite = ((row + row_half) % row_count, col)
+
+    everyone = [target(move, (core + phase) % 2) for phase in range(2) for move in moves] + [sibling]
+    barrier = pltpu.get_barrier_semaphore()
+    for device, _, _ in everyone:
+        pl.semaphore_signal(barrier, inc=1, device_id=device, device_id_type=MESH)
+    pl.semaphore_signal(barrier, inc=1, device_id=opposite, device_id_type=MESH)
+    pl.semaphore_wait(barrier, len(everyone) + 1)
+
+    def remote(source, destination, send_sem, recv_sem, device):
+        return pltpu.make_async_remote_copy(
+            src_ref=source,
+            dst_ref=destination,
+            send_sem=send_sem,
+            recv_sem=recv_sem,
+            device_id=device,
+            device_id_type=MESH,
+        )
+
+    def begin(copy):
+        copy.start()
+        return copy
+
+    table_copies = [
+        begin(remote(table_hbm.at[place], tables.at[mine], table_send.at[number], table_recv.at[number], device))
+        for device, place, number in everyone
+    ]
+    own_table = pltpu.make_async_copy(table_hbm.at[mine], tables.at[mine], own_sems.at[0])
+    own_table.start()
+    for load in loads:
+        load.wait()
+
+    def fill(base, slots, destination, at, lead=0):
+        unit = min(4, slots)
+
+        def some(step, _):
+            for k in range(unit):
+                slot = step * unit + k
+                packed = slot_ref[base + slot]
+                source, panel_at = packed // (2 * rows_of_panel), packed // 2 % rows_of_panel
+                product = block_product(sparse[source], panel[panel_at])
+                before = destination[at + jnp.maximum(slot - 1, -lead)]
+                destination[at + slot] = product + jnp.where(packed % 2 > 0, before, 0.0)
+            return 0
+
+        lax.fori_loop(0, slots // unit, some, 0)
+
+    def direct(base, index, land, send, recv, number, device):
+        at = base + index * per_owner
+        fill(at, per_owner, products, at)
+        return begin(
+            remote(
+                products.at[pl.ds(at, per_owner)],
+                land.at[pl.ds(mine * per_owner, per_owner)],
+                send.at[number],
+                recv.at[number],
+                device,
+            )
+        )
+
+    def send_far(device, place, number):
+        return direct(far_base, place, far_land, far_send, far_recv, number, device)
+
+    def send_near(device, place, number):
+        return direct(near_base, place % around, near_land, near_send, near_recv, number, device)
+
+    def send_list(first, land, index):
+        slots = land.shape[0]
+        fill(list_base + first, slots, products, list_base + first, min(first, 1))
+        return remote(
+            products.at[pl.ds(list_base + first, slots)], land, list_send.at[index], list_recv.at[index], partner
+        )
+
+    far_copies = [send_far(*target(move, core)) for move in moves]
+    list_one_copy = begin(send_list(0, list_one, 0))
+    far_copies += [send_far(*target(move, (core + 1) % 2)) for move in flat_moves]
+    far_copies.append(send_far(*sibling))
+    fill(far_base + mine * per_owner, per_owner, far_land, mine * per_owner)
+    list_two_copy = send_list(first_list, list_two, 1)
+
+    @pl.when(core == 1)
+    def _():
+        list_two_copy.start()
+
+    near_targets = [target(move, (core + phase) % 2) for phase in range(2) for move in flat_moves] + [sibling]
+    near_copies = [send_near(*one) for one in near_targets]
+    fill(near_base + mine % around * per_owner, per_owner, near_land, mine * per_owner)
+
+    own_table.wait()
+    for copy in table_copies:
+        copy.wait_recv()
+    lookups = [
+        pltpu.make_async_copy(tables.at[:, 0, :], near_table, own_sems.at[1]),
+        pltpu.make_async_copy(tables.at[:, 1, :], far_table, own_sems.at[2]),
+        pltpu.make_async_copy(tables.at[:, 2, :], starts, own_sems.at[3]),
+    ]
+    for lookup in lookups:
+        lookup.start()
+    worst = tables[0]
+    for origin in range(1, count):
+        worst = jnp.maximum(worst, tables[origin])
+    spill[...] = worst
+    spill_copy = begin(remote(spill, spill_in, spill_sems.at[0], spill_sems.at[1], opposite))
+    for lookup in lookups:
+        lookup.wait()
+
+    def reduce(land, table, destination, first, number):
+        def one(step, _):
+            column = first + step
+            value = land[table[0, column]]
+            for origin in range(1, count):
+                value = value + land[table[origin, column]]
+            destination[column] = value
+            return 0
+
+        lax.fori_loop(0, number, one, 0)
+
+    cross_copies = [
+        remote(
+            sums.at[pl.ds(index * chunk, chunk)],
+            crossed.at[pl.ds(index * chunk, chunk)],
+            cross_send.at[index],
+            cross_recv.at[index],
+            opposite,
+        )
+        for index in range(chunks)
+    ]
+
+    def cross():
+        for index in range(chunks):
+            reduce(far_land, far_table, sums, index * chunk, chunk)
+            cross_copies[index].start()
+
+    straight = [target(move, (core + phase) % 2) for phase in range(2) for move in flat_moves] + [sibling]
+    level = lambda number, recv: remote(
+        products.at[pl.ds(0, per_owner)],
+        far_land.at[pl.ds(mine * per_owner, per_owner)],
+        far_send.at[0],
+        recv.at[number],
+        partner,
+    )
+
+    def await_level():
+        for _, _, number in straight:
+            level(number, far_recv).wait_recv()
+
+    @pl.when(core == 0)
+    def _():
+        await_level()
+        for number in range(around, count):
+            level(number, far_recv).wait_recv()
+        cross()
+        list_two_copy.start()
+
+    relayed = []
+
+    def relay(index, starting, land, shift, both):
+        def pull(place, destination, at):
+            start = starts[partner_place, starting(place % around)]
+
+            def one(k, _):
+                where = start + k
+                value = list_one[jnp.minimum(where, first_list - 1)]
+                if both:
+                    other = list_two[jnp.clip(where - first_list, 0, second_list - 1)]
+                    value = jnp.where(where < first_list, value, other)
+                destination[at + k] = value
+                return 0
+
+            lax.fori_loop(0, per_owner, one, 0)
+
+        def push(device, place, number):
+            at = shift + place % around * per_owner
+            pull(place, sparse, at)
+            return begin(
+                remote(
+                    sparse.at[pl.ds(at, per_owner)],
+                    land.at[pl.ds(partner_place * per_owner, per_owner)],
+                    pass_send.at[index * around + number],
+                    pass_recv.at[index * around + number],
+                    device,
+                )
+            )
+
+        def keep():
+            pull(mine, land, partner_place * per_owner)
+
+        return push, keep
+
+    push_far, keep_far = relay(0, lambda place: place // 2, far_land, 0, False)
+    push_near, keep_near = relay(
+        1, lambda place: around // 2 + place, near_land, around * per_owner, True
+    )
+    sibling_pass = lambda index, land: remote(
+        sparse.at[pl.ds(0, per_owner)],
+        land.at[pl.ds(partner_place * per_owner, per_owner)],
+        pass_send.at[index * around + 1],
+        pass_recv.at[index * around + 1],
+        sibling[0],
+    )
+
+    list_one_copy.wait_recv()
+    far_passes = [push_far(*target(move, (core + 1) % 2)) for move in flat_moves]
+
+    @pl.when(core == 0)
+    def _():
+        push_far(*sibling)
+
+    @pl.when(core == 1)
+    def _():
+        keep_far()
+        await_level()
+        for _, _, number in straight:
+            level(number, pass_recv).wait_recv()
+        cross()
+
+    list_two_copy.wait_recv()
+    near_passes = [push_near(*one) for one in near_targets]
+    keep_near()
+
+    spill_copy.wait_recv()
+    flag_ref[...] = jnp.maximum(spill[...], spill_in[...])
+    for copy in near_copies + near_passes:
+        copy.wait_recv()
+    reduce(near_land, near_table, total, 0, local_blocks)
+    outs = []
+    for index, copy in enumerate(cross_copies):
+        copy.wait_recv()
+        part = pl.ds(index * chunk, chunk)
+        total[part] = total[part] + crossed[part]
+        out = pltpu.make_async_copy(total.at[part], out_hbm.at[part], out_sems.at[index])
+        out.start()
+        outs.append(out)
+    sent = table_copies + far_copies + [list_one_copy, list_two_copy] + near_copies
+    for copy in sent + far_passes + near_passes + cross_copies + [spill_copy]:
+        copy.wait_send()
+
+    @pl.when(core == 0)
+    def _():
+        sibling_pass(0, far_land).wait_send()
+
+    for out in outs:
+        out.wait()
+
+
+def route_layers(slots, sparse_blocks, panel_blocks, table, row_half, per_owner, first_list, list_slots):
+    count = row_half * lax.axis_size("col")
+    around = count // 2
+    local_blocks, size, width = panel_blocks.shape
+    half_slots = count * per_owner
+    chunks = local_blocks // min(8, local_blocks)
+    lanes = table.shape[-1]
+    scalars = pl.BlockSpec(memory_space=pltpu.SMEM)
+    anywhere = pl.BlockSpec(memory_space=pl.ANY)
+    block = (size, width)
+    dma = pltpu.SemaphoreType.DMA
+    blocks = lambda number: pltpu.VMEM((number,) + block, jnp.float32)
+    return pl.pallas_call(
+        functools.partial(layer_kernel, row_half, per_owner, first_list),
+        in_specs=[scalars] + [anywhere] * 3,
+        out_specs=[anywhere, pl.BlockSpec(memory_space=pltpu.VMEM)],
+        out_shape=[
+            jax.ShapeDtypeStruct((local_blocks,) + block, jnp.float32),
+            jax.ShapeDtypeStruct((TILE, lanes), jnp.int32),
+        ],
+        scratch_shapes=[
+            pltpu.VMEM(sparse_blocks.shape, jnp.float32),
+            pltpu.VMEM(panel_blocks.shape, jnp.float32),
+            blocks(around * per_owner + half_slots + list_slots),
+            blocks(half_slots + 1),
+            blocks(half_slots + 1),
+            blocks(first_list),
+            blocks(list_slots - first_list),
+            blocks(local_blocks),
+            blocks(local_blocks),
+            blocks(local_blocks),
+            pltpu.VMEM((count, TILE, lanes), jnp.int32),
+            pltpu.VMEM((TILE, lanes), jnp.int32),
+            pltpu.VMEM((TILE, lanes), jnp.int32),
+            pltpu.SMEM((count, lanes), jnp.int32),
+            pltpu.SMEM((count, lanes), jnp.int32),
+            pltpu.SMEM((count, lanes), jnp.int32),
+            dma((count,)),
+            dma((count,)),
+            dma((around,)),
+            dma((around,)),
+            dma((2 * around,)),
+            dma((2 * around,)),
+            dma((2,)),
+            dma((2,)),
+            dma((count,)),
+            dma((count,)),
+            dma((chunks,)),
+            dma((chunks,)),
+            dma((2,)),
+            dma((2,)),
+            dma((4,)),
+            dma((chunks,)),
+        ],
+        compiler_params=pltpu.CompilerParams(
+            collective_id=1, has_side_effects=True, vmem_limit_bytes=VMEM_LIMIT
+        ),
+    )(slots, sparse_blocks, panel_blocks, table)
+
+
 def body(sparse_blocks, panel_rows, block_row, block_owner, block_offset):
     device_count = lax.axis_size("row") * lax.axis_size("col")
     half_count = device_count // 2
@@ -290,25 +683,62 @@
     earlier = same & (key[None, :] < key[:, None])
     order = jnp.sum(earlier.astype(jnp.int32), axis=1)
     again = jnp.any(earlier & (block_offset[None, :] == block_offset[:, None]), axis=1).astype(jnp.int32)
-    half_of = (owner // half_count != my_half).astype(jnp.int32)
-    group = half_of * half_count + owner % half_count
-    position = group * per_owner + order
-    hit = position[None, :] == jnp.arange(2 * half_slots, dtype=jnp.int32)[:, None]
-    pick = lambda value: jnp.max(jnp.where(hit, value[None, :], 0), axis=1)
-    source, panel_at, keep = pick(index), pick(block_row), pick(again)
-
-    lanes = -(-local_blocks // LANES) * LANES
-    place = (me % half_count) * per_owner + order
+    far = (owner // half_count != my_half).astype(jnp.int32)
+    place = owner % half_count
+    panel_blocks = panel_rows.reshape(local_blocks, size, width)
+    lanes = -(-max(local_blocks, LANES) // LANES) * LANES
+
+    landing = (me % half_count) * per_owner + order
+    group = far * half_count + place
     cell = (group[None, :] == jnp.arange(2 * half_count, dtype=jnp.int32)[:, None])[:, None, :] & (
         block_offset[None, :] == jnp.arange(lanes, dtype=jnp.int32)[:, None]
     )[None]
-    table = jnp.max(jnp.where(cell, place[None, None, :], -1), axis=2)
-    table = jnp.where(table < 0, half_slots, table)
-    table = table.reshape(2, half_count, 1, lanes).transpose(1, 0, 2, 3)
-    table = jnp.broadcast_to(table, (half_count, 2, TILE, lanes)).reshape(half_count, 2 * TILE, lanes)
-
-    panel_blocks = panel_rows.reshape(local_blocks, size, width)
-    total = route(source, panel_at, keep, sparse_blocks, panel_blocks, table, row_half, per_owner)
+    table = jnp.max(jnp.where(cell, landing[None, None, :], -1), axis=2)
+    table = jnp.where(table < 0, half_slots, table).reshape(2, half_count, 1, lanes)
+
+    def whole():
+        position = group * per_owner + order
+        hit = position[None, :] == jnp.arange(2 * half_slots, dtype=jnp.int32)[:, None]
+        pick = lambda value: jnp.max(jnp.where(hit, value[None, :], 0), axis=1)
+        pair = table.transpose(1, 0, 2, 3)
+        pair = jnp.broadcast_to(pair, (half_count, 2, TILE, lanes)).reshape(half_count, 2 * TILE, lanes)
+        return route(
+            pick(index), pick(block_row), pick(again), sparse_blocks, panel_blocks, pair, row_half, per_owner
+        )
+
+    lower = min(2, row_half)
+    around = lower * lax.axis_size("col")
+    if half_count != 2 * around or local_blocks < 8:
+        return whole().reshape(local_blocks * size, width)
+
+    first_list = around // 2 * per_owner
+    list_slots = max(slot_count // 2, first_list + 8)
+    beyond = place // around != (me % half_count) // around
+    flat_place = place % around
+    listed = beyond & ((far == 0) | (flat_place % 2 == 1))
+    list_group = jnp.where(far == 1, flat_place // 2, around // 2 + flat_place)
+    list_group = jnp.where(listed, list_group, lanes)
+    ahead = jnp.sum((list_group[None, :] < list_group[:, None]).astype(jnp.int32), axis=1)
+    starts = jnp.sum(
+        (list_group[None, :] < jnp.arange(lanes, dtype=jnp.int32)[:, None]).astype(jnp.int32), axis=1
+    )
+    spilled = jnp.sum(listed.astype(jnp.int32)) > list_slots
+    starts = jnp.where(jnp.arange(lanes) == lanes - 1, jnp.where(spilled, SPILL, 0), starts)
+    list_base = around * per_owner + half_slots
+    position = jnp.where(
+        listed,
+        list_base + ahead + order,
+        jnp.where(far == 1, around * per_owner + place * per_owner + order, flat_place * per_owner + order),
+    )
+    packed = (index * local_blocks + block_row) * 2 + again
+    hit = position[None, :] == jnp.arange(list_base + list_slots, dtype=jnp.int32)[:, None]
+    slots = jnp.max(jnp.where(hit, packed[None, :], 0), axis=1)
+    kind = jnp.arange(TILE, dtype=jnp.int32)[None, :, None]
+    rows = jnp.where(kind == 0, table[0], jnp.where(kind == 1, table[1], starts[None, None, :]))
+    total, flags = route_layers(
+        slots, sparse_blocks, panel_blocks, rows, row_half, per_owner, first_list, list_slots
+    )
+    total = lax.cond(flags[2, lanes - 1] >= SPILL, whole, lambda: total)
     return total.reshape(local_blocks * size, width)
 
 

time: 299 us -> 284 us (0.950)
  Pallas kernels: 288 us -> 268 us
    pallas_call x1, Pallas kernels: 288 us -> 268 us  [route_layers(): pl.pallas_call(functools.partial(layer_kernel, row_half, per_owner, first...]
where the time goes in v1:
time: 284 us
  Pallas kernels  268 us (94%)
  other arithmetic  7.37 us (3%)
  local copies, waits for them, and re-layouts  6.76 us (2%)
    pallas_call x1, Pallas kernels, route_layers(): pl.pallas_call(functools.partial(layer_kernel, row_half, per_owner, first...  268 us

profile of v1, /device:TPU:1, one launch (start us, length us, event | category | flops | bytes accessed | tf_op | source)
XLA Modules:
  0.0 284.1 jit_solution(3334413735299028751)
XLA Ops:
  0.0 0.7 iota_add_fusion
  0.7 0.9 convert_reduce_fusion.1
  1.6 0.7 fusion.3
  2.3 0.7 select_add_fusion
  2.9 0.6 convert_reduce_fusion.3
  4.3 0.2 convert_reduce_fusion
  4.5 0.9 iota_compare_fusion.3
  5.4 0.6 select_reduce_fusion.3
  6.0 0.7 multiply_add_fusion.1
  6.7 0.7 select_reduce_fusion.4.slot_ref
  7.4 0.5 broadcast.490
  7.9 0.5 rem.155
  8.4 0.7 select_select_fusion.table_hbm
  9.1 0.0 copy-start
  9.1 268.4 %shard_map.57 = (f32[64,128,128]{2,1,0:T(8,128)}, s32[8,128]{1,0:T(8,128)}) custom-call(s32[256]{0:T(256)} %select_reduce_fusion.4.slot_ref, f32[128,128,128]{2,1,0:T(8,128)} %sparse_hbm.1, f32[64,128,128]{2,1,0:T(8,128)} %bitcast.22, s32[16,8,128]{2,1,0:T(8,128)} %select_select_fusion.table_hbm), custom_call_target="tpu_custom_call" | custom-call | tf_op jit(solution)/shard_map/pallas_call | solution.py:620
  277.5 1.3 slice.13
  279.5 0.0 copy-done
  279.5 0.2 conditional.1
  279.7 4.5 %copy.14 = f32[8192,128]{1,0:T(8,128)} copy(f32[8192,128]{1,0:T(8,128)} %get-tuple-element.82) | data formatting | bytes 8388608
  (8 shorter events, 0.1 us)
Async XLA Ops:
  9.1 270.4 %copy-start = (s32[128]{0:T(128)S(1)}, s32[128]{0:T(128)}, u32[]{:S(2)}) copy-start(s32[128]{0:T(128)} %param.9) | copy-start | bytes 1540

commit v2 on v1

--- a/solution.py
+++ b/solution.py
@@ -315,9 +315,11 @@
     load_sems,
     own_sems,
     out_sems,
+    beside_sems,
+    across_sems,
 ):
     row, col = lax.axis_index("row"), lax.axis_index("col")
-    row_count, col_count = lax.axis_size("row"), lax.axis_size("col")
+    col_count = lax.axis_size("col")
     half, inner = row // row_half, row % row_half
     outer, core = col // 2, col % 2
     lower = min(2, row_half)
@@ -360,14 +362,15 @@
     sibling = target(still, 1)
     partner_inner = (layer + 1) % 2 * lower + beside_x
     partner, partner_place = (half * row_half + partner_inner, col), partner_inner * col_count + col
-    opposite = ((row + row_half) % row_count, col)
+    opposite = ((1 - half) * row_half + (1 - layer) * lower + beside_x, col)
 
     everyone = [target(move, (core + phase) % 2) for phase in range(2) for move in moves] + [sibling]
     barrier = pltpu.get_barrier_semaphore()
     for device, _, _ in everyone:
         pl.semaphore_signal(barrier, inc=1, device_id=device, device_id_type=MESH)
     pl.semaphore_signal(barrier, inc=1, device_id=opposite, device_id_type=MESH)
-    pl.semaphore_wait(barrier, len(everyone) + 1)
+    with jax.named_scope("barrier"):
+        pl.semaphore_wait(barrier, len(everyone) + 1)
 
     def remote(source, destination, send_sem, recv_sem, device):
         return pltpu.make_async_remote_copy(
@@ -389,8 +392,9 @@
     ]
     own_table = pltpu.make_async_copy(table_hbm.at[mine], tables.at[mine], own_sems.at[0])
     own_table.start()
-    for load in loads:
-        load.wait()
+    with jax.named_scope("load_wait"):
+        for load in loads:
+            load.wait()
 
     def fill(base, slots, destination, at, lead=0):
         unit = min(4, slots)
@@ -407,24 +411,26 @@
 
         lax.fori_loop(0, slots // unit, some, 0)
 
-    def direct(base, index, land, send, recv, number, device):
+    def direct(base, index, land, send, recv, number, device, later=False):
         at = base + index * per_owner
+        copy = remote(
+            products.at[pl.ds(at, per_owner)],
+            land.at[pl.ds(mine * per_owner, per_owner)],
+            send.at[number],
+            recv.at[number],
+            device,
+        )
+
         fill(at, per_owner, products, at)
-        return begin(
-            remote(
-                products.at[pl.ds(at, per_owner)],
-                land.at[pl.ds(mine * per_owner, per_owner)],
-                send.at[number],
-                recv.at[number],
-                device,
-            )
-        )
+        if not later:
+            copy.start()
+        return copy
 
     def send_far(device, place, number):
         return direct(far_base, place, far_land, far_send, far_recv, number, device)
 
     def send_near(device, place, number):
-        return direct(near_base, place % around, near_land, near_send, near_recv, number, device)
+        return direct(near_base, place % around, near_land, near_send, near_recv, number, device, True)
 
     def send_list(first, land, index):
         slots = land.shape[0]
@@ -433,24 +439,32 @@
             products.at[pl.ds(list_base + first, slots)], land, list_send.at[index], list_recv.at[index], partner
         )
 
-    far_copies = [send_far(*target(move, core)) for move in moves]
-    list_one_copy = begin(send_list(0, list_one, 0))
-    far_copies += [send_far(*target(move, (core + 1) % 2)) for move in flat_moves]
-    far_copies.append(send_far(*sibling))
-    fill(far_base + mine * per_owner, per_owner, far_land, mine * per_owner)
-    list_two_copy = send_list(first_list, list_two, 1)
-
-    @pl.when(core == 1)
-    def _():
-        list_two_copy.start()
+    with jax.named_scope("far_first"):
+        far_copies = [send_far(*target(move, core)) for move in moves]
+    with jax.named_scope("list_one"):
+        list_one_copy = begin(send_list(0, list_one, 0))
+    with jax.named_scope("far_second"):
+        far_copies += [send_far(*target(move, (core + 1) % 2)) for move in flat_moves]
+        far_copies.append(send_far(*sibling))
+        fill(far_base + mine * per_owner, per_owner, far_land, mine * per_owner)
+    with jax.named_scope("list_two"):
+        list_two_copy = send_list(first_list, list_two, 1)
+
+    at_end = layer == half
 
     near_targets = [target(move, (core + phase) % 2) for phase in range(2) for move in flat_moves] + [sibling]
-    near_copies = [send_near(*one) for one in near_targets]
-    fill(near_base + mine % around * per_owner, per_owner, near_land, mine * per_owner)
-
-    own_table.wait()
-    for copy in table_copies:
-        copy.wait_recv()
+    with jax.named_scope("near_own"):
+        near_copies = [send_near(*one) for one in near_targets]
+        fill(near_base + mine % around * per_owner, per_owner, near_land, mine * per_owner)
+
+    def start_near():
+        for copy in near_copies:
+            copy.start()
+
+    with jax.named_scope("table_wait"):
+        own_table.wait()
+        for copy in table_copies:
+            copy.wait_recv()
     lookups = [
         pltpu.make_async_copy(tables.at[:, 0, :], near_table, own_sems.at[1]),
         pltpu.make_async_copy(tables.at[:, 1, :], far_table, own_sems.at[2]),
@@ -488,10 +502,11 @@
         for index in range(chunks)
     ]
 
-    def cross():
+    def cross(held=False):
         for index in range(chunks):
             reduce(far_land, far_table, sums, index * chunk, chunk)
-            cross_copies[index].start()
+            if not held:
+                cross_copies[index].start()
 
     straight = [target(move, (core + phase) % 2) for phase in range(2) for move in flat_moves] + [sibling]
     level = lambda number, recv: remote(
@@ -508,13 +523,19 @@
 
     @pl.when(core == 0)
     def _():
-        await_level()
-        for number in range(around, count):
-            level(number, far_recv).wait_recv()
-        cross()
-        list_two_copy.start()
-
-    relayed = []
+        with jax.named_scope("far_wait"):
+            await_level()
+            for number in range(around, count):
+                level(number, far_recv).wait_recv()
+        @pl.when(at_end)
+        def _():
+            with jax.named_scope("cross_early"):
+                cross(True)
+
+        @pl.when(jnp.logical_not(at_end))
+        def _():
+            with jax.named_scope("cross_early"):
+                cross()
 
     def relay(index, starting, land, shift, both):
         def pull(place, destination, at):
@@ -561,40 +582,94 @@
         sibling[0],
     )
 
-    list_one_copy.wait_recv()
-    far_passes = [push_far(*target(move, (core + 1) % 2)) for move in flat_moves]
+    with jax.named_scope("list_one_wait"):
+        list_one_copy.wait_recv()
+
+    @pl.when(jnp.logical_not(at_end))
+    def _():
+        list_two_copy.start()
+    with jax.named_scope("pass_far"):
+        far_passes = [push_far(*target(move, (core + 1) % 2)) for move in flat_moves]
 
     @pl.when(core == 0)
     def _():
         push_far(*sibling)
 
+    @pl.when(at_end & (core == 1))
+    def _():
+        pl.semaphore_signal(beside_sems.at[0], inc=1, device_id=sibling[0], device_id_type=MESH)
+
+    @pl.when(at_end & (core == 0))
+    def _():
+        pl.semaphore_wait(beside_sems.at[0], 1)
+        pl.semaphore_signal(across_sems.at[0], inc=1, device_id=opposite, device_id_type=MESH)
+        pl.semaphore_wait(across_sems.at[0], 1)
+        for copy in cross_copies:
+            copy.start()
+        list_two_copy.start()
+
+    start_near()
+
     @pl.when(core == 1)
     def _():
         keep_far()
-        await_level()
-        for _, _, number in straight:
-            level(number, pass_recv).wait_recv()
-        cross()
-
-    list_two_copy.wait_recv()
-    near_passes = [push_near(*one) for one in near_targets]
-    keep_near()
-
-    spill_copy.wait_recv()
-    flag_ref[...] = jnp.maximum(spill[...], spill_in[...])
-    for copy in near_copies + near_passes:
-        copy.wait_recv()
-    reduce(near_land, near_table, total, 0, local_blocks)
+        with jax.named_scope("pass_far_wait"):
+            await_level()
+            for _, _, number in straight:
+                level(number, pass_recv).wait_recv()
+
+        @pl.when(at_end)
+        def _():
+            list_two_copy.start()
+            with jax.named_scope("cross_late"):
+                cross(True)
+
+        @pl.when(jnp.logical_not(at_end))
+        def _():
+            with jax.named_scope("cross_late"):
+                cross()
+
+    with jax.named_scope("list_two_wait"):
+        list_two_copy.wait_recv()
+    with jax.named_scope("pass_near"):
+        near_passes = [push_near(*one) for one in near_targets]
+        keep_near()
+
+    @pl.when(at_end & (core == 0))
+    def _():
+        pl.semaphore_signal(beside_sems.at[1], inc=1, device_id=sibling[0], device_id_type=MESH)
+
+    @pl.when(at_end & (core == 1))
+    def _():
+        pl.semaphore_wait(beside_sems.at[1], 1)
+        pl.semaphore_signal(across_sems.at[1], inc=1, device_id=opposite, device_id_type=MESH)
+        pl.semaphore_wait(across_sems.at[1], 1)
+        for copy in cross_copies:
+            copy.start()
+
+
+    spill_copy.wait()
+    spill[...] = jnp.maximum(spill[...], spill_in[...])
+    flag_copy = pltpu.make_async_copy(spill.at[2], starts.at[0], own_sems.at[0])
+    flag_copy.start()
+    flag_copy.wait()
+    flag_ref[0, 0] = starts[0, starts.shape[1] - 1]
+    with jax.named_scope("near_wait"):
+        for copy in near_copies + near_passes:
+            copy.wait_recv()
+    with jax.named_scope("near_sum"):
+        reduce(near_land, near_table, total, 0, local_blocks)
     outs = []
     for index, copy in enumerate(cross_copies):
-        copy.wait_recv()
+        with jax.named_scope(f"cross_wait{index}"):
+            copy.wait_recv()
         part = pl.ds(index * chunk, chunk)
         total[part] = total[part] + crossed[part]
         out = pltpu.make_async_copy(total.at[part], out_hbm.at[part], out_sems.at[index])
         out.start()
         outs.append(out)
     sent = table_copies + far_copies + [list_one_copy, list_two_copy] + near_copies
-    for copy in sent + far_passes + near_passes + cross_copies + [spill_copy]:
+    for copy in sent + far_passes + near_passes + cross_copies:
         copy.wait_send()
 
     @pl.when(core == 0)
@@ -620,10 +695,10 @@
     return pl.pallas_call(
         functools.partial(layer_kernel, row_half, per_owner, first_list),
         in_specs=[scalars] + [anywhere] * 3,
-        out_specs=[anywhere, pl.BlockSpec(memory_space=pltpu.VMEM)],
+        out_specs=[anywhere, scalars],
         out_shape=[
             jax.ShapeDtypeStruct((local_blocks,) + block, jnp.float32),
-            jax.ShapeDtypeStruct((TILE, lanes), jnp.int32),
+            jax.ShapeDtypeStruct((1, 1), jnp.int32),
         ],
         scratch_shapes=[
             pltpu.VMEM(sparse_blocks.shape, jnp.float32),
@@ -658,6 +733,8 @@
             dma((2,)),
             dma((4,)),
             dma((chunks,)),
+            pltpu.SemaphoreType.REGULAR((2,)),
+            pltpu.SemaphoreType.REGULAR((2,)),
         ],
         compiler_params=pltpu.CompilerParams(
             collective_id=1, has_side_effects=True, vmem_limit_bytes=VMEM_LIMIT
@@ -688,19 +765,20 @@
     panel_blocks = panel_rows.reshape(local_blocks, size, width)
     lanes = -(-max(local_blocks, LANES) // LANES) * LANES
 
-    landing = (me % half_count) * per_owner + order
-    group = far * half_count + place
-    cell = (group[None, :] == jnp.arange(2 * half_count, dtype=jnp.int32)[:, None])[:, None, :] & (
-        block_offset[None, :] == jnp.arange(lanes, dtype=jnp.int32)[:, None]
-    )[None]
-    table = jnp.max(jnp.where(cell, landing[None, None, :], -1), axis=2)
-    table = jnp.where(table < 0, half_slots, table).reshape(2, half_count, 1, lanes)
+    def tables(group):
+        landing = (me % half_count) * per_owner + order
+        cell = (group[None, :] == jnp.arange(2 * half_count, dtype=jnp.int32)[:, None])[:, None, :] & (
+            block_offset[None, :] == jnp.arange(lanes, dtype=jnp.int32)[:, None]
+        )[None]
+        table = jnp.max(jnp.where(cell, landing[None, None, :], -1), axis=2)
+        return jnp.where(table < 0, half_slots, table).reshape(2, half_count, 1, lanes)
 
     def whole():
+        group = far * half_count + owner % half_count
         position = group * per_owner + order
         hit = position[None, :] == jnp.arange(2 * half_slots, dtype=jnp.int32)[:, None]
         pick = lambda value: jnp.max(jnp.where(hit, value[None, :], 0), axis=1)
-        pair = table.transpose(1, 0, 2, 3)
+        pair = tables(group).transpose(1, 0, 2, 3)
         pair = jnp.broadcast_to(pair, (half_count, 2, TILE, lanes)).reshape(half_count, 2 * TILE, lanes)
         return route(
             pick(index), pick(block_row), pick(again), sparse_blocks, panel_blocks, pair, row_half, per_owner
@@ -713,6 +791,8 @@
 
     first_list = around // 2 * per_owner
     list_slots = max(slot_count // 2, first_list + 8)
+    place = jnp.where(far == 1, (place + around) % half_count, place)
+    table = tables(far * half_count + place)
     beyond = place // around != (me % half_count) // around
     flat_place = place % around
     listed = beyond & ((far == 0) | (flat_place % 2 == 1))
@@ -738,7 +818,7 @@
     total, flags = route_layers(
         slots, sparse_blocks, panel_blocks, rows, row_half, per_owner, first_list, list_slots
     )
-    total = lax.cond(flags[2, lanes - 1] >= SPILL, whole, lambda: total)
+    total = lax.cond(flags[0, 0] >= SPILL, whole, lambda: total)
     return total.reshape(local_blocks * size, width)
 
 

time: 284 us -> 260 us (0.915)
  Pallas kernels: 268 us -> 246 us
    pallas_call x1, Pallas kernels: 268 us -> 246 us  [route_layers(): pl.pallas_call(functools.partial(layer_kernel, row_half, per_owner, first...]
where the time goes in v2:
time: 260 us
  Pallas kernels  246 us (95%)
  other arithmetic  7.41 us (3%)
  local copies, waits for them, and re-layouts  4.49 us (2%)
    pallas_call x1, Pallas kernels, route_layers(): pl.pallas_call(functools.partial(layer_kernel, row_half, per_owner, first...  246 us

profile of v2, /device:TPU:1, one launch (start us, length us, event | category | flops | bytes accessed | tf_op | source)
XLA Modules:
  0.0 259.8 jit_solution(17696642578922077620)
XLA Ops:
  0.0 0.7 iota_add_fusion
  0.7 0.9 convert_reduce_fusion.1
  1.6 0.7 fusion.7
  2.3 0.7 fusion.4
  3.0 0.6 convert_reduce_fusion.3
  4.3 0.2 convert_reduce_fusion
  4.5 0.9 iota_compare_fusion.5
  5.4 0.6 select_reduce_fusion.4
  6.1 0.7 multiply_add_fusion.1
  6.8 0.7 select_reduce_fusion.5.slot_ref
  7.4 0.7 select_select_fusion.table_hbm
  8.1 0.0 copy-start
  8.1 0.0 copy-start.1
  8.1 0.0 copy-start.2
  8.1 246.4 %shard_map.57 = (f32[64,128,128]{2,1,0:T(8,128)}, s32[1,1]{1,0:T(1,128)}) custom-call(s32[256]{0:T(256)} %select_reduce_fusion.5.slot_ref, f32[128,128,128]{2,1,0:T(8,128)} %sparse_hbm.1, f32[64,128,128]{2,1,0:T(8,128)} %bitcast.21, s32[16,8,128]{2,1,0:T(8,128)} %select_select_fusion.table_hbm), custom_call_target="tpu_custom_call" | custom-call | tf_op jit(solution)/shard_map/pallas_call | solution.py:695
  255.1 0.0 copy-done
  255.1 0.0 copy-done.1
  255.1 0.0 copy-done.2
  255.1 0.2 conditional.1
  255.3 4.5 %copy.14 = f32[8192,128]{1,0:T(8,128)} copy(f32[8192,128]{1,0:T(8,128)} %get-tuple-element.45) | data formatting | bytes 8388608
  (8 shorter events, 0.1 us)
Async XLA Ops:
  8.1 247.0 %copy-start = (s32[128,1]{0,1:T(1,128)S(1)}, s32[128,1]{0,1:T(1,128)}, u32[]{:S(2)}) copy-start(s32[128,1]{0,1:T(1,128)} %param.10) | copy-start | bytes 1540
  8.1 247.0 %copy-start.1 = (s32[128]{0:T(128)S(1)}, s32[128]{0:T(128)}, u32[]{:S(2)}) copy-start(s32[128]{0:T(128)} %param.11) | copy-start | bytes 1540
  8.1 247.0 %copy-start.2 = (s32[128]{0:T(128)S(1)}, s32[128]{0:T(128)}, u32[]{:S(2)}) copy-start(s32[128]{0:T(128)} %param.9) | copy-start | bytes 1540

commit v3 on v2

--- a/solution.py
+++ b/solution.py
@@ -11,7 +11,6 @@
 VMEM_LIMIT = 67_000_000
 LANES = 128
 TILE = 8
-SPILL = 1 << 20
 MESH = pl.DeviceIdType.MESH
 
 
@@ -273,14 +272,62 @@
     )(source, panel_at, keep, sparse_blocks, panel_blocks, table)
 
 
+def prepare(items_ref, made, slots_made, half, mine, per_owner, count, around, local_blocks, list_slots):
+    slots = items_ref.shape[1]
+    across = jnp.broadcast_to(items_ref[...], (slots, slots))
+    down = jnp.transpose(across)
+    lane = lax.broadcasted_iota(jnp.int32, (slots, LANES), 1)
+    item = lax.broadcasted_iota(jnp.int32, (slots, LANES), 0)
+    half_slots = count * per_owner
+
+    def parts(packed):
+        offset = packed // local_blocks % local_blocks
+        owner = packed // (local_blocks * local_blocks)
+        far = owner // count != half
+        place = jnp.where(far, (owner + around) % count, owner % count)
+        flat = place % around
+        listed = (place // around != mine // around) & (jnp.logical_not(far) | (flat % 2 == 1))
+        list_group = jnp.where(listed, jnp.where(far, flat // 2, around // 2 + flat), LANES)
+        return owner, offset, far, place, flat, listed, list_group
+
+    owner_r, offset_r, _, _, _, _, list_group_r = parts(across)
+    owner_c, offset_c, far_c, place_c, flat_c, listed_c, list_group_c = parts(down)
+    key_r, key_c = offset_r * slots + lane, offset_c * slots + item
+    earlier = (owner_r == owner_c) & (key_r < key_c)
+    total = lambda mask, value: jnp.sum(jnp.where(mask, value, 0), axis=1, keepdims=True)
+    ranked = total(earlier, jnp.where(offset_r == offset_c, slots + 1, 1))
+    order, again = jnp.minimum(ranked % slots, per_owner - 1), jnp.minimum(ranked // slots, 1)
+    ahead = total(list_group_r < list_group_c, 1)
+    position = jnp.where(
+        listed_c,
+        around * per_owner + half_slots + ahead + order,
+        jnp.where(far_c, around * per_owner + place_c * per_owner + order, flat_c * per_owner + order),
+    )
+    packed = (item * local_blocks + down % local_blocks) * 2 + again
+    for block in range(slots_made.shape[0]):
+        picked = jnp.max(jnp.where(position == lane + block * LANES, packed, 0), axis=0, keepdims=True)
+        slots_made[pl.ds(block, 1), :] = picked
+    starts = jnp.sum((list_group_c < lane).astype(jnp.int32), axis=0, keepdims=True)
+    landing = jnp.where(offset_c == lane, mine * per_owner + order, -1)
+    kind = lax.broadcasted_iota(jnp.int32, (TILE, LANES), 0)
+
+    def table(far, index):
+        own = (far_c == far) & (place_c == index)
+        best = jnp.max(jnp.where(own, landing, -1), axis=0, keepdims=True)
+        return jnp.where(best < 0, half_slots, best)
+
+    for index in range(count):
+        near, away = table(False, index), table(True, index)
+        made[index] = jnp.where(kind == 0, near, jnp.where(kind == 1, away, starts))
+
+
 def layer_kernel(
     row_half,
     per_owner,
     first_list,
-    slot_ref,
+    items_ref,
     sparse_hbm,
     panel_hbm,
-    table_hbm,
     out_hbm,
     flag_ref,
     sparse,
@@ -294,6 +341,9 @@
     crossed,
     total,
     tables,
+    made,
+    slots_made,
+    slot_ref,
     spill,
     spill_in,
     near_table,
@@ -369,6 +419,13 @@
     for device, _, _ in everyone:
         pl.semaphore_signal(barrier, inc=1, device_id=device, device_id_type=MESH)
     pl.semaphore_signal(barrier, inc=1, device_id=opposite, device_id_type=MESH)
+
+    with jax.named_scope("prepare"):
+        prepare(
+            items_ref, made, slots_made, half, mine, per_owner, count, around, local_blocks, first_list + second_list
+        )
+        slot_copy = pltpu.make_async_copy(slots_made, slot_ref, own_sems.at[4])
+        slot_copy.start()
     with jax.named_scope("barrier"):
         pl.semaphore_wait(barrier, len(everyone) + 1)
 
@@ -387,11 +444,12 @@
         return copy
 
     table_copies = [
-        begin(remote(table_hbm.at[place], tables.at[mine], table_send.at[number], table_recv.at[number], device))
+        begin(remote(made.at[place], tables.at[mine], table_send.at[number], table_recv.at[number], device))
         for device, place, number in everyone
     ]
-    own_table = pltpu.make_async_copy(table_hbm.at[mine], tables.at[mine], own_sems.at[0])
+    own_table = pltpu.make_async_copy(made.at[mine], tables.at[mine], own_sems.at[0])
     own_table.start()
+    slot_copy.wait()
     with jax.named_scope("load_wait"):
         for load in loads:
             load.wait()
@@ -402,7 +460,7 @@
         def some(step, _):
             for k in range(unit):
                 slot = step * unit + k
-                packed = slot_ref[base + slot]
+                packed = slot_ref[(base + slot) // LANES, (base + slot) % LANES]
                 source, panel_at = packed // (2 * rows_of_panel), packed // 2 % rows_of_panel
                 product = block_product(sparse[source], panel[panel_at])
                 before = destination[at + jnp.maximum(slot - 1, -lead)]
@@ -680,13 +738,14 @@
         out.wait()
 
 
-def route_layers(slots, sparse_blocks, panel_blocks, table, row_half, per_owner, first_list, list_slots):
+def route_layers(items, sparse_blocks, panel_blocks, row_half, per_owner, first_list, list_slots):
     count = row_half * lax.axis_size("col")
     around = count // 2
     local_blocks, size, width = panel_blocks.shape
     half_slots = count * per_owner
     chunks = local_blocks // min(8, local_blocks)
-    lanes = table.shape[-1]
+    lanes = LANES
+    made_slots = around * per_owner + half_slots + list_slots
     scalars = pl.BlockSpec(memory_space=pltpu.SMEM)
     anywhere = pl.BlockSpec(memory_space=pl.ANY)
     block = (size, width)
@@ -694,7 +753,7 @@
     blocks = lambda number: pltpu.VMEM((number,) + block, jnp.float32)
     return pl.pallas_call(
         functools.partial(layer_kernel, row_half, per_owner, first_list),
-        in_specs=[scalars] + [anywhere] * 3,
+        in_specs=[pl.BlockSpec(memory_space=pltpu.VMEM)] + [anywhere] * 2,
         out_specs=[anywhere, scalars],
         out_shape=[
             jax.ShapeDtypeStruct((local_blocks,) + block, jnp.float32),
@@ -712,6 +771,9 @@
             blocks(local_blocks),
             blocks(local_blocks),
             pltpu.VMEM((count, TILE, lanes), jnp.int32),
+            pltpu.VMEM((count, TILE, lanes), jnp.int32),
+            pltpu.VMEM((-(-made_slots // lanes), lanes), jnp.int32),
+            pltpu.SMEM((-(-made_slots // lanes), lanes), jnp.int32),
             pltpu.VMEM((TILE, lanes), jnp.int32),
             pltpu.VMEM((TILE, lanes), jnp.int32),
             pltpu.SMEM((count, lanes), jnp.int32),
@@ -731,7 +793,7 @@
             dma((chunks,)),
             dma((2,)),
             dma((2,)),
-            dma((4,)),
+            dma((5,)),
             dma((chunks,)),
             pltpu.SemaphoreType.REGULAR((2,)),
             pltpu.SemaphoreType.REGULAR((2,)),
@@ -739,7 +801,7 @@
         compiler_params=pltpu.CompilerParams(
             collective_id=1, has_side_effects=True, vmem_limit_bytes=VMEM_LIMIT
         ),
-    )(slots, sparse_blocks, panel_blocks, table)
+    )(items, sparse_blocks, panel_blocks)
 
 
 def body(sparse_blocks, panel_rows, block_row, block_owner, block_offset):
@@ -754,31 +816,28 @@
     my_half = me // half_count
     row_half = lax.axis_size("row") // 2
     owner = block_owner[:, 0]
-    index = jnp.arange(slot_count, dtype=jnp.int32)
-    key = block_offset * slot_count + index
-    same = owner[:, None] == owner[None, :]
-    earlier = same & (key[None, :] < key[:, None])
-    order = jnp.sum(earlier.astype(jnp.int32), axis=1)
-    again = jnp.any(earlier & (block_offset[None, :] == block_offset[:, None]), axis=1).astype(jnp.int32)
-    far = (owner // half_count != my_half).astype(jnp.int32)
-    place = owner % half_count
     panel_blocks = panel_rows.reshape(local_blocks, size, width)
     lanes = -(-max(local_blocks, LANES) // LANES) * LANES
 
-    def tables(group):
+    def whole():
+        index = jnp.arange(slot_count, dtype=jnp.int32)
+        key = block_offset * slot_count + index
+        same = owner[:, None] == owner[None, :]
+        earlier = same & (key[None, :] < key[:, None])
+        order = jnp.sum(earlier.astype(jnp.int32), axis=1)
+        again = jnp.any(earlier & (block_offset[None, :] == block_offset[:, None]), axis=1).astype(jnp.int32)
+        far = (owner // half_count != my_half).astype(jnp.int32)
+        group = far * half_count + owner % half_count
         landing = (me % half_count) * per_owner + order
         cell = (group[None, :] == jnp.arange(2 * half_count, dtype=jnp.int32)[:, None])[:, None, :] & (
             block_offset[None, :] == jnp.arange(lanes, dtype=jnp.int32)[:, None]
         )[None]
         table = jnp.max(jnp.where(cell, landing[None, None, :], -1), axis=2)
-        return jnp.where(table < 0, half_slots, table).reshape(2, half_count, 1, lanes)
-
-    def whole():
-        group = far * half_count + owner % half_count
+        table = jnp.where(table < 0, half_slots, table).reshape(2, half_count, 1, lanes)
         position = group * per_owner + order
         hit = position[None, :] == jnp.arange(2 * half_slots, dtype=jnp.int32)[:, None]
         pick = lambda value: jnp.max(jnp.where(hit, value[None, :], 0), axis=1)
-        pair = tables(group).transpose(1, 0, 2, 3)
+        pair = table.transpose(1, 0, 2, 3)
         pair = jnp.broadcast_to(pair, (half_count, 2, TILE, lanes)).reshape(half_count, 2 * TILE, lanes)
         return route(
             pick(index), pick(block_row), pick(again), sparse_blocks, panel_blocks, pair, row_half, per_owner
@@ -786,39 +845,14 @@
 
     lower = min(2, row_half)
     around = lower * lax.axis_size("col")
-    if half_count != 2 * around or local_blocks < 8:
+    if half_count != 2 * around or slot_count != LANES or not 8 <= local_blocks < LANES:
         return whole().reshape(local_blocks * size, width)
 
     first_list = around // 2 * per_owner
     list_slots = max(slot_count // 2, first_list + 8)
-    place = jnp.where(far == 1, (place + around) % half_count, place)
-    table = tables(far * half_count + place)
-    beyond = place // around != (me % half_count) // around
-    flat_place = place % around
-    listed = beyond & ((far == 0) | (flat_place % 2 == 1))
-    list_group = jnp.where(far == 1, flat_place // 2, around // 2 + flat_place)
-    list_group = jnp.where(listed, list_group, lanes)
-    ahead = jnp.sum((list_group[None, :] < list_group[:, None]).astype(jnp.int32), axis=1)
-    starts = jnp.sum(
-        (list_group[None, :] < jnp.arange(lanes, dtype=jnp.int32)[:, None]).astype(jnp.int32), axis=1
-    )
-    spilled = jnp.sum(listed.astype(jnp.int32)) > list_slots
-    starts = jnp.where(jnp.arange(lanes) == lanes - 1, jnp.where(spilled, SPILL, 0), starts)
-    list_base = around * per_owner + half_slots
-    position = jnp.where(
-        listed,
-        list_base + ahead + order,
-        jnp.where(far == 1, around * per_owner + place * per_owner + order, flat_place * per_owner + order),
-    )
-    packed = (index * local_blocks + block_row) * 2 + again
-    hit = position[None, :] == jnp.arange(list_base + list_slots, dtype=jnp.int32)[:, None]
-    slots = jnp.max(jnp.where(hit, packed[None, :], 0), axis=1)
-    kind = jnp.arange(TILE, dtype=jnp.int32)[None, :, None]
-    rows = jnp.where(kind == 0, table[0], jnp.where(kind == 1, table[1], starts[None, None, :]))
-    total, flags = route_layers(
-        slots, sparse_blocks, panel_blocks, rows, row_half, per_owner, first_list, list_slots
-    )
-    total = lax.cond(flags[0, 0] >= SPILL, whole, lambda: total)
+    items = ((owner * local_blocks + block_offset) * local_blocks + block_row).reshape(1, slot_count)
+    total, flags = route_layers(items, sparse_blocks, panel_blocks, row_half, per_owner, first_list, list_slots)
+    total = lax.cond(flags[0, 0] > list_slots, whole, lambda: total)
     return total.reshape(local_blocks * size, width)
 
 

time: 260 us -> 253 us (0.973)
  other arithmetic: 7.41 us -> 1.2 us
where the time goes in v3:
time: 253 us
  Pallas kernels  246 us (97%)
  local copies, waits for them, and re-layouts  4.48 us (2%)
    pallas_call x1, Pallas kernels, route_layers(): pl.pallas_call(functools.partial(layer_kernel, row_half, per_owner, first...  246 us

profile of v3, /device:TPU:1, one launch (start us, length us, event | category | flops | bytes accessed | tf_op | source)
XLA Modules:
  0.0 252.8 jit_solution(14628555985595903430)
XLA Ops:
  0.0 1.2 add_bitcast_fusion.items_ref
  1.2 0.0 copy-start
  1.2 0.0 copy-start.1
  1.2 0.0 copy-start.2
  1.2 246.3 %shard_map.58 = (f32[64,128,128]{2,1,0:T(8,128)}, s32[1,1]{1,0:T(1,128)}) custom-call(s32[1,128]{1,0:T(1,128)} %add_bitcast_fusion.items_ref, f32[128,128,128]{2,1,0:T(8,128)} %sparse_hbm.1, f32[64,128,128]{2,1,0:T(8,128)} %bitcast.21), custom_call_target="tpu_custom_call" | custom-call | tf_op jit(solution)/shard_map/pallas_call | solution.py:754
  248.1 0.0 copy-done
  248.1 0.0 copy-done.1
  248.1 0.0 copy-done.2
  248.1 0.2 conditional.1
  248.3 4.5 %copy.16 = f32[8192,128]{1,0:T(8,128)} copy(f32[8192,128]{1,0:T(8,128)} %get-tuple-element.39) | data formatting | bytes 8388608
Async XLA Ops:
  1.2 246.9 %copy-start = (s32[128,1]{0,1:T(1,128)S(1)}, s32[128,1]{0,1:T(1,128)}, u32[]{:S(2)}) copy-start(s32[128,1]{0,1:T(1,128)} %param.10) | copy-start | bytes 1540
  1.2 246.9 %copy-start.1 = (s32[128]{0:T(128)S(1)}, s32[128]{0:T(128)}, u32[]{:S(2)}) copy-start(s32[128]{0:T(128)} %param.11) | copy-start | bytes 1540
  1.2 246.9 %copy-start.2 = (s32[128]{0:T(128)S(1)}, s32[128]{0:T(128)}, u32[]{:S(2)}) copy-start(s32[128]{0:T(128)} %param.9) | copy-start | bytes 1540

commit v4 on v3

--- a/solution.py
+++ b/solution.py
@@ -272,9 +272,10 @@
     )(source, panel_at, keep, sparse_blocks, panel_blocks, table)
 
 
-def prepare(items_ref, made, slots_made, half, mine, per_owner, count, around, local_blocks, list_slots):
-    slots = items_ref.shape[1]
-    across = jnp.broadcast_to(items_ref[...], (slots, slots))
+def prepare(owner_ref, offset_ref, row_ref, made, slots_made, half, mine, per_owner, count, around, local_blocks, list_slots):
+    slots = owner_ref.shape[1]
+    items = (owner_ref[...] * local_blocks + offset_ref[...]) * local_blocks + row_ref[...]
+    across = jnp.broadcast_to(items, (slots, slots))
     down = jnp.transpose(across)
     lane = lax.broadcasted_iota(jnp.int32, (slots, LANES), 1)
     item = lax.broadcasted_iota(jnp.int32, (slots, LANES), 0)
@@ -325,7 +326,9 @@
     row_half,
     per_owner,
     first_list,
-    items_ref,
+    owner_ref,
+    offset_ref,
+    row_ref,
     sparse_hbm,
     panel_hbm,
     out_hbm,
@@ -334,7 +337,8 @@
     panel,
     products,
     far_land,
-    near_land,
+    near_own,
+    near_pass,
     list_one,
     list_two,
     sums,
@@ -394,7 +398,8 @@
         load.start()
     blank = jnp.zeros(far_land.shape[1:], jnp.float32)
     far_land[half_slots] = blank
-    near_land[half_slots] = blank
+    near_own[around * per_owner] = blank
+    near_pass[around * per_owner] = blank
 
     def target(move_pair, flip):
         one, other = move_pair
@@ -422,7 +427,18 @@
 
     with jax.named_scope("prepare"):
         prepare(
-            items_ref, made, slots_made, half, mine, per_owner, count, around, local_blocks, first_list + second_list
+            owner_ref,
+            offset_ref,
+            row_ref,
+            made,
+            slots_made,
+            half,
+            mine,
+            per_owner,
+            count,
+            around,
+            local_blocks,
+            first_list + second_list,
         )
         slot_copy = pltpu.make_async_copy(slots_made, slot_ref, own_sems.at[4])
         slot_copy.start()
@@ -469,11 +485,11 @@
 
         lax.fori_loop(0, slots // unit, some, 0)
 
-    def direct(base, index, land, send, recv, number, device, later=False):
+    def direct(base, index, land, spot, send, recv, number, device, later=False):
         at = base + index * per_owner
         copy = remote(
             products.at[pl.ds(at, per_owner)],
-            land.at[pl.ds(mine * per_owner, per_owner)],
+            land.at[pl.ds(spot * per_owner, per_owner)],
             send.at[number],
             recv.at[number],
             device,
@@ -485,10 +501,10 @@
         return copy
 
     def send_far(device, place, number):
-        return direct(far_base, place, far_land, far_send, far_recv, number, device)
+        return direct(far_base, place, far_land, mine, far_send, far_recv, number, device)
 
     def send_near(device, place, number):
-        return direct(near_base, place % around, near_land, near_send, near_recv, number, device, True)
+        return direct(near_base, place % around, near_own, mine % around, near_send, near_recv, number, device, True)
 
     def send_list(first, land, index):
         slots = land.shape[0]
@@ -498,7 +514,7 @@
         )
 
     with jax.named_scope("far_first"):
-        far_copies = [send_far(*target(move, core)) for move in moves]
+        far_copies = [send_far(*target(move, core)) for move in sorted(moves, key=lambda pair: -pair[0][0] - pair[1][0])]
     with jax.named_scope("list_one"):
         list_one_copy = begin(send_list(0, list_one, 0))
     with jax.named_scope("far_second"):
@@ -513,7 +529,7 @@
     near_targets = [target(move, (core + phase) % 2) for phase in range(2) for move in flat_moves] + [sibling]
     with jax.named_scope("near_own"):
         near_copies = [send_near(*one) for one in near_targets]
-        fill(near_base + mine % around * per_owner, per_owner, near_land, mine * per_owner)
+        fill(near_base + mine % around * per_owner, per_owner, near_own, mine % around * per_owner)
 
     def start_near():
         for copy in near_copies:
@@ -595,7 +611,7 @@
             with jax.named_scope("cross_early"):
                 cross()
 
-    def relay(index, starting, land, shift, both):
+    def relay(index, starting, land, spot, shift, both):
         def pull(place, destination, at):
             start = starts[partner_place, starting(place % around)]
 
@@ -616,7 +632,7 @@
             return begin(
                 remote(
                     sparse.at[pl.ds(at, per_owner)],
-                    land.at[pl.ds(partner_place * per_owner, per_owner)],
+                    land.at[pl.ds(spot * per_owner, per_owner)],
                     pass_send.at[index * around + number],
                     pass_recv.at[index * around + number],
                     device,
@@ -624,13 +640,13 @@
             )
 
         def keep():
-            pull(mine, land, partner_place * per_owner)
+            pull(mine, land, spot * per_owner)
 
         return push, keep
 
-    push_far, keep_far = relay(0, lambda place: place // 2, far_land, 0, False)
+    push_far, keep_far = relay(0, lambda place: place // 2, far_land, partner_place, 0, False)
     push_near, keep_near = relay(
-        1, lambda place: around // 2 + place, near_land, around * per_owner, True
+        1, lambda place: around // 2 + place, near_pass, mine % around, around * per_owner, True
     )
     sibling_pass = lambda index, land: remote(
         sparse.at[pl.ds(0, per_owner)],
@@ -712,11 +728,28 @@
     flag_copy.start()
     flag_copy.wait()
     flag_ref[0, 0] = starts[0, starts.shape[1] - 1]
+    def gather_near(land, at_layer, begun):
+        limit = around * per_owner
+
+        def one(column, _):
+            value = total[column] if begun else blank
+            for step in range(around):
+                spot = near_table[at_layer * around + step, column] - at_layer * limit
+                value = value + land[jnp.minimum(spot, limit)]
+            total[column] = value
+            return 0
+
+        lax.fori_loop(0, local_blocks, one, 0)
+
+    with jax.named_scope("near_own_wait"):
+        for copy in near_copies:
+            copy.wait_recv()
+    gather_near(near_own, layer, False)
     with jax.named_scope("near_wait"):
-        for copy in near_copies + near_passes:
+        for copy in near_passes:
             copy.wait_recv()
     with jax.named_scope("near_sum"):
-        reduce(near_land, near_table, total, 0, local_blocks)
+        gather_near(near_pass, 1 - layer, True)
     outs = []
     for index, copy in enumerate(cross_copies):
         with jax.named_scope(f"cross_wait{index}"):
@@ -738,7 +771,7 @@
         out.wait()
 
 
-def route_layers(items, sparse_blocks, panel_blocks, row_half, per_owner, first_list, list_slots):
+def route_layers(owner, offset, block_row, sparse_blocks, panel_blocks, row_half, per_owner, first_list, list_slots):
     count = row_half * lax.axis_size("col")
     around = count // 2
     local_blocks, size, width = panel_blocks.shape
@@ -753,7 +786,7 @@
     blocks = lambda number: pltpu.VMEM((number,) + block, jnp.float32)
     return pl.pallas_call(
         functools.partial(layer_kernel, row_half, per_owner, first_list),
-        in_specs=[pl.BlockSpec(memory_space=pltpu.VMEM)] + [anywhere] * 2,
+        in_specs=[pl.BlockSpec(memory_space=pltpu.VMEM)] * 3 + [anywhere] * 2,
         out_specs=[anywhere, scalars],
         out_shape=[
             jax.ShapeDtypeStruct((local_blocks,) + block, jnp.float32),
@@ -764,7 +797,8 @@
             pltpu.VMEM(panel_blocks.shape, jnp.float32),
             blocks(around * per_owner + half_slots + list_slots),
             blocks(half_slots + 1),
-            blocks(half_slots + 1),
+            blocks(around * per_owner + 1),
+            blocks(around * per_owner + 1),
             blocks(first_list),
             blocks(list_slots - first_list),
             blocks(local_blocks),
@@ -801,7 +835,7 @@
         compiler_params=pltpu.CompilerParams(
             collective_id=1, has_side_effects=True, vmem_limit_bytes=VMEM_LIMIT
         ),
-    )(items, sparse_blocks, panel_blocks)
+    )(owner, offset, block_row, sparse_blocks, panel_blocks)
 
 
 def body(sparse_blocks, panel_rows, block_row, block_owner, block_offset):
@@ -850,8 +884,18 @@
 
     first_list = around // 2 * per_owner
     list_slots = max(slot_count // 2, first_list + 8)
-    items = ((owner * local_blocks + block_offset) * local_blocks + block_row).reshape(1, slot_count)
-    total, flags = route_layers(items, sparse_blocks, panel_blocks, row_half, per_owner, first_list, list_slots)
+    as_row = lambda value: value.reshape(1, slot_count)
+    total, flags = route_layers(
+        as_row(block_owner),
+        as_row(block_offset),
+        as_row(block_row),
+        sparse_blocks,
+        panel_blocks,
+        row_half,
+        per_owner,
+        first_list,
+        list_slots,
+    )
     total = lax.cond(flags[0, 0] > list_slots, whole, lambda: total)
     return total.reshape(local_blocks * size, width)
 

time: 253 us -> 249 us (0.984)
  Pallas kernels: 246 us -> 243 us
    pallas_call x1, Pallas kernels: 246 us -> 243 us  [route_layers(): pl.pallas_call(functools.partial(layer_kernel, row_half, per_owner, first...]
where the time goes in v4:
time: 249 us
  Pallas kernels  243 us (98%)
  local copies, waits for them, and re-layouts  4.48 us (2%)
    pallas_call x1, Pallas kernels, route_layers(): pl.pallas_call(functools.partial(layer_kernel, row_half, per_owner, first...  243 us

profile of v4, /device:TPU:1, one launch (start us, length us, event | category | flops | bytes accessed | tf_op | source)
XLA Modules:
  0.0 248.7 jit_solution(13807879205482518835)
XLA Ops:
  0.0 0.0 copy-start
  0.0 0.0 copy-start.1
  0.0 0.0 copy-start.2
  0.0 243.4 %shard_map.58 = (f32[64,128,128]{2,1,0:T(8,128)}, s32[1,1]{1,0:T(1,128)}) custom-call(s32[1,128]{1,0:T(1,128)} %bitcast.34, s32[1,128]{1,0:T(1,128)} %bitcast.37, s32[1,128]{1,0:T(1,128)} %bitcast.38, f32[128,128,128]{2,1,0:T(8,128)} %sparse_hbm.1, f32[64,128,128]{2,1,0:T(8,128)} %bitcast.29), custom_call_target="tpu_custom_call" | custom-call | tf_op jit(solution)/shard_map/pallas_call | solution.py:787
  244.1 0.0 copy-done
  244.1 0.0 copy-done.1
  244.1 0.0 copy-done.2
  244.1 0.2 conditional.1
  244.3 4.5 %copy.15 = f32[8192,128]{1,0:T(8,128)} copy(f32[8192,128]{1,0:T(8,128)} %get-tuple-element.39) | data formatting | bytes 8388608
Async XLA Ops:
  0.0 244.1 %copy-start = (s32[128,1]{0,1:T(1,128)S(1)}, s32[128,1]{0,1:T(1,128)}, u32[]{:S(2)}) copy-start(s32[128,1]{0,1:T(1,128)} %param.10) | copy-start | bytes 1540
  0.0 244.1 %copy-start.1 = (s32[128]{0:T(128)S(1)}, s32[128]{0:T(128)}, u32[]{:S(2)}) copy-start(s32[128]{0:T(128)} %param.11) | copy-start | bytes 1540
  0.0 244.1 %copy-start.2 = (s32[128]{0:T(128)S(1)}, s32[128]{0:T(128)}, u32[]{:S(2)}) copy-start(s32[128]{0:T(128)} %param.9) | copy-start | bytes 1540

commit v5 on v4

--- a/solution.py
+++ b/solution.py
@@ -659,7 +659,9 @@
     with jax.named_scope("list_one_wait"):
         list_one_copy.wait_recv()
 
-    @pl.when(jnp.logical_not(at_end))
+    in_turn = jnp.logical_not(at_end) & (core == 0)
+
+    @pl.when(in_turn)
     def _():
         list_two_copy.start()
     with jax.named_scope("pass_far"):
@@ -703,12 +705,18 @@
             with jax.named_scope("cross_late"):
                 cross()
 
+    @pl.when(in_turn)
+    def _():
+        list_two_copy.wait_send()
+        pl.semaphore_signal(beside_sems.at[0], inc=1, device_id=sibling[0], device_id_type=MESH)
+
+    @pl.when(jnp.logical_not(at_end) & (core == 1))
+    def _():
+        pl.semaphore_wait(beside_sems.at[0], 1)
+        list_two_copy.start()
+
     with jax.named_scope("list_two_wait"):
         list_two_copy.wait_recv()
-    with jax.named_scope("pass_near"):
-        near_passes = [push_near(*one) for one in near_targets]
-        keep_near()
-
     @pl.when(at_end & (core == 0))
     def _():
         pl.semaphore_signal(beside_sems.at[1], inc=1, device_id=sibling[0], device_id_type=MESH)
@@ -720,6 +728,10 @@
         pl.semaphore_wait(across_sems.at[1], 1)
         for copy in cross_copies:
             copy.start()
+
+    with jax.named_scope("pass_near"):
+        near_passes = [push_near(*one) for one in near_targets]
+        keep_near()
 
 
     spill_copy.wait()
@@ -759,9 +771,13 @@
         out = pltpu.make_async_copy(total.at[part], out_hbm.at[part], out_sems.at[index])
         out.start()
         outs.append(out)
-    sent = table_copies + far_copies + [list_one_copy, list_two_copy] + near_copies
+    sent = table_copies + far_copies + [list_one_copy] + near_copies
     for copy in sent + far_passes + near_passes + cross_copies:
         copy.wait_send()
+
+    @pl.when(jnp.logical_not(in_turn))
+    def _():
+        list_two_copy.wait_send()
 
     @pl.when(core == 0)
     def _():

time: 249 us -> 249 us (level)
  no operation moved by 1% of the time
where the time goes in v5:
time: 249 us
  Pallas kernels  243 us (98%)
  local copies, waits for them, and re-layouts  4.48 us (2%)
    pallas_call x1, Pallas kernels, route_layers(): pl.pallas_call(functools.partial(layer_kernel, row_half, per_owner, first...  243 us

profile of v5, /device:TPU:1, one launch (start us, length us, event | category | flops | bytes accessed | tf_op | source)
XLA Modules:
  0.0 248.6 jit_solution(4097396886867266630)
XLA Ops:
  0.0 0.0 copy-start
  0.0 0.0 copy-start.1
  0.0 0.0 copy-start.2
  0.0 243.3 %shard_map.58 = (f32[64,128,128]{2,1,0:T(8,128)}, s32[1,1]{1,0:T(1,128)}) custom-call(s32[1,128]{1,0:T(1,128)} %bitcast.34, s32[1,128]{1,0:T(1,128)} %bitcast.37, s32[1,128]{1,0:T(1,128)} %bitcast.38, f32[128,128,128]{2,1,0:T(8,128)} %sparse_hbm.1, f32[64,128,128]{2,1,0:T(8,128)} %bitcast.29), custom_call_target="tpu_custom_call" | custom-call | tf_op jit(solution)/shard_map/pallas_call | solution.py:803
  243.9 0.0 copy-done
  244.0 0.0 copy-done.1
  244.0 0.0 copy-done.2
  244.0 0.2 conditional.1
  244.2 4.5 %copy.15 = f32[8192,128]{1,0:T(8,128)} copy(f32[8192,128]{1,0:T(8,128)} %get-tuple-element.39) | data formatting | bytes 8388608
Async XLA Ops:
  0.0 243.9 %copy-start = (s32[128,1]{0,1:T(1,128)S(1)}, s32[128,1]{0,1:T(1,128)}, u32[]{:S(2)}) copy-start(s32[128,1]{0,1:T(1,128)} %param.10) | copy-start | bytes 1540
  0.0 244.0 %copy-start.1 = (s32[128]{0:T(128)S(1)}, s32[128]{0:T(128)}, u32[]{:S(2)}) copy-start(s32[128]{0:T(128)} %param.11) | copy-start | bytes 1540
  0.0 244.0 %copy-start.2 = (s32[128]{0:T(128)S(1)}, s32[128]{0:T(128)}, u32[]{:S(2)}) copy-start(s32[128]{0:T(128)} %param.9) | copy-start | bytes 1540
